TPU v7x, 32 devices: a whole 2x2x4 slice. The times are simulated.
32 devices in a mesh: seq: 8 (over z, y), head: 4 (over x, core).
Axes of the slice: x: 2, y: 2, z: 4, core: 2. Of those that a mesh axis runs over, the one named last changes fastest.
Arguments:
- inputs: bfloat16 [2048, 5120], P('seq', 'head'), may hold values from -6 to 6
- time_step: float32 [80, 2048], P('head', 'seq'), may hold values from 0.01 to 0.3
- decay_rate: float32 [80], P('head'), may hold values from 0.0001 to 1
- input_map: bfloat16 [2048, 128], P('seq'), may hold values from -6 to 6
- output_map: bfloat16 [2048, 128], P('seq'), may hold values from -0.59765625 to 0.59765625
- output_grad: bfloat16 [2048, 5120], P('seq', 'head'), may hold values from -3 to 3
- span_states: float32 [8, 80, 64, 128], P('seq', 'head'), may hold values from -6 to 6
- resets: int32 [8], P('seq'), may hold values from 0 to 4095
Outputs:
- grad_inputs: bfloat16 [2048, 5120], P('seq', 'head')
- grad_input_map: float32 [2048, 128], P('seq')
- grad_rate: float32 [80], P('head')
Inputs may be any that keep to these rules, and one draw needn't show every extreme that they name: `resets`: A value p under 256 means that a document starts at position p of that span; a value of 256 or more means that none starts in it.
All inputs are finite; a program needn't handle non-finite values.
Results may differ from a plain program's by a relative error of at most 0.003.
Values sent between devices are 32-bit elements; how exact they have to be, the bound alone decides.
A program may use at most 64 MiB of HBM per device.

v0:
```python
import jax
import jax.numpy as jnp
from jax import lax
from jax.sharding import PartitionSpec as P

highest = lax.Precision.HIGHEST


def prepare(x_block, step_block, decay_rate, b_block, c_block, grad_block, start_state, reset_at):
    block_len = step_block.shape[1]
    positions = jnp.arange(block_len, dtype=jnp.int32)
    later_doc = positions >= reset_at
    no_reset = reset_at >= block_len
    elapsed = jnp.cumsum(step_block, axis=1)
    log_decay = -decay_rate[:, None] * elapsed
    joined = (later_doc[:, None] == later_doc[None, :]) & (positions[None, :] >= positions[:, None])
    log_gaps = log_decay[:, None, :] - log_decay[:, :, None]
    pair_weight = jnp.where(joined[None], jnp.exp(jnp.where(joined[None], log_gaps, 0.0)), 0.0)
    intersection = jnp.dot(b_block, c_block.T, preferred_element_type=jnp.float32)
    products = jnp.einsum("shp,uhp->hsu", x_block, grad_block, preferred_element_type=jnp.float32)
    mixing = (pair_weight * intersection[None]).astype(jnp.bfloat16)
    pair_terms = pair_weight * products
    paired = pair_terms.astype(jnp.bfloat16)
    dx_inner = jnp.einsum("hsu,uhp->shp", mixing, grad_block, preferred_element_type=jnp.float32)
    db_inner = jnp.einsum("hsu,un->hsn", paired, c_block, preferred_element_type=jnp.float32)
    start_weight = jnp.where(later_doc[None], 0.0, jnp.exp(log_decay))
    end_weight = jnp.where(
        (later_doc | no_reset)[None], jnp.exp(log_decay[:, -1:] - log_decay), 0.0
    )
    carry_gain = jnp.where(no_reset, jnp.exp(log_decay[:, -1]), 0.0)
    c_wide = c_block.astype(jnp.float32)
    grad_wide = grad_block.astype(jnp.float32)
    weighted_c = start_weight[:, :, None] * c_wide[None]
    boundary_grad = jnp.einsum("hun,uhp->hpn", weighted_c, grad_wide, precision=highest)
    state_read = jnp.einsum("uhp,hpn->hun", grad_wide, start_state, precision=highest)
    start_term = jnp.sum(state_read * c_wide[None], axis=2)
    inside_term = jnp.sum(
        pair_terms
        * intersection[None]
        * step_block[:, :, None]
        * (elapsed[:, None, :] - elapsed[:, :, None]),
        axis=(1, 2),
    )
    entry_term = jnp.sum(start_weight * elapsed * start_term, axis=1)
    return (
        carry_gain,
        boundary_grad,
        dx_inner,
        db_inner,
        inside_term + entry_term,
        end_weight,
        elapsed,
    )


def finish(prepared, x_block, step_block, b_block, start_state, carried):
    carry_gain, boundary_grad, dx_inner, db_inner, partial_rate, end_weight, elapsed = prepared
    b_wide = b_block.astype(jnp.float32)
    x_wide = x_block.astype(jnp.float32)
    carried_b = jnp.einsum("sn,hpn->shp", b_wide, carried, precision=highest)
    carried_x = jnp.einsum("shp,hpn->hsn", x_wide, carried, precision=highest)
    step_rows = step_block.T[:, :, None]
    end_rows = end_weight.T[:, :, None]
    grad_x = (step_rows * (dx_inner + end_rows * carried_b)).astype(jnp.bfloat16)
    grad_b = jnp.sum(
        step_block[:, :, None] * (db_inner + end_weight[:, :, None] * carried_x), axis=0
    )
    last_elapsed = elapsed[:, -1]
    leaving_term = jnp.sum(
        end_weight
        * step_block
        * (last_elapsed[:, None] - elapsed)
        * jnp.sum(carried_x * b_wide[None], axis=2),
        axis=1,
    )
    through_term = carry_gain * last_elapsed * jnp.sum(carried * start_state, axis=(1, 2))
    return (grad_x, grad_b, partial_rate + leaving_term + through_term)


def backward_step(running, members):
    grad_piece, gain_piece = members
    return (grad_piece + gain_piece[:, None] * running, running)


def body(inputs, time_step, decay_rate, input_map, output_map, output_grad, span_states, resets):
    length = time_step.shape[1]
    block_count = span_states.shape[0]
    block_len = length // block_count
    head_count = decay_rate.shape[0]
    head_width = inputs.shape[1] // head_count
    number = 0
    x_block = inputs.reshape(block_len, head_count, head_width)
    grad_block = output_grad.reshape(block_len, head_count, head_width)
    step_block = time_step
    b_block = input_map
    prepared = prepare(
        x_block,
        step_block,
        decay_rate,
        b_block,
        output_map,
        grad_block,
        span_states[number],
        resets[number],
    )
    pieces = [(prepared, x_block, step_block, b_block)]
    gain_total = jnp.ones((head_count,), jnp.float32)
    grad_total = jnp.zeros_like(span_states[0])
    for number in reversed(range(block_count)):
        gain_block, grad_block_sum = (pieces[number][0][0], pieces[number][0][1])
        grad_total = grad_block_sum + gain_block[:, None, None] * grad_total
        gain_total = gain_block * gain_total
    seq_count = lax.axis_size("seq")
    entries = grad_total.shape[1] * grad_total.shape[2]
    sliced = grad_total.reshape(head_count, seq_count, entries // seq_count)
    received = lax.all_to_all(sliced, "seq", split_axis=1, concat_axis=1, tiled=True)
    gains = lax.all_gather(gain_total[None], "seq", axis=0, tiled=True)
    ending, exclusive = lax.scan(
        backward_step,
        jnp.zeros_like(received[:, 0]),
        (jnp.transpose(received, (1, 0, 2)), gains),
        reverse=True,
    )
    returned = lax.all_to_all(
        jnp.transpose(exclusive, (1, 0, 2)), "seq", split_axis=1, concat_axis=1, tiled=True
    )
    incoming = returned.reshape(grad_total.shape)
    carried = incoming
    grad_x_list = [None] * block_count
    grad_b_list = [None] * block_count
    rate_total = jnp.zeros((head_count,), jnp.float32)
    for number in reversed(range(block_count)):
        prepared, x_block, step_block, b_block = pieces[number]
        grad_x, grad_b, rate_part = finish(
            prepared, x_block, step_block, b_block, span_states[number], carried
        )
        grad_x_list[number] = grad_x.reshape(block_len, head_count * head_width)
        grad_b_list[number] = grad_b
        rate_total = rate_part
        carried = prepared[1] + prepared[0][:, None, None] * carried
    grad_inputs = grad_x_list[0]
    grad_input_map = lax.psum(grad_b_list[0], "head")
    grad_rate = -lax.psum(rate_total, "seq")
    return (grad_inputs, grad_input_map, grad_rate)


def solution(mesh):
    in_specs = (
        P("seq", "head"),
        P("head", "seq"),
        P("head"),
        P("seq", None),
        P("seq", None),
        P("seq", "head"),
        P("seq", "head", None, None),
        P("seq"),
    )
    out_specs = (P("seq", "head"), P("seq", None), P("head"))
    return jax.shard_map(body, mesh=mesh, in_specs=in_specs, out_specs=out_specs, check_vma=False)
```

profile of v0, /device:TPU:0, one launch (start us, length us, event | category | flops | bytes accessed | tf_op | source)
XLA Modules:
  0.0 141.0 jit_solution(17333116644024165966)
XLA Ops:
  8.6 0.8 reshape.290
  11.2 0.9 copy.37
  12.2 1.4 copy.36
  13.6 1.7 %fusion.31 = f32[20,64,128]{2,1,0:T(8,128)S(1)} fusion(bf16[256,20,64]{0,2,1:T(8,128)(2,1)S(1)} %bitcast.80, f32[256,128]{0,1:T(8,128)S(1)} %copy.37, f32[20,256]{1,0:T(8,128)S(1)} %get-tuple-element.152, f32[20]{0:T(128)S(1)} %broadcast_multiply_fusion.1), kind=kOutput, calls=%fused_computation.38 | convolution fusion | flops 504135680 | bytes 1462352 | tf_op jit(solution)/shard_map/hun,uhp->hpn/dot_general | solution.py:34
  15.4 1.3 copy.39
  16.7 7.3 %all-to-all-start = ((f32[20,8,1024]{2,0,1:T(8,128)}), f32[20,8,1024]{2,0,1:T(8,128)S(1)}, u32[]{:S(2)}, u32[]{:S(2)}) async-start(f32[20,8,1024]{2,0,1:T(8,128)} %copy.39), calls=%async_computation | async-start | bytes 1572864 | tf_op jit(solution)/shard_map/all_to_all | solution.py:116
  25.6 26.1 %all-reduce = f32[160]{0:T(256)S(1)} all-reduce(f32[160]{0:T(256)S(1)} %dynamic-update-slice), channel_id=2, replica_groups=mesh['seq'=8,'head'=4] {'seq'}, use_global_device_ids=true, to_apply=%add | all-reduce | flops 160 | bytes 1280
  53.9 0.7 slice_reduce_fusion.1
  54.7 1.4 %fusion.37 = pred[256,256]{1,0:T(8,128)(4,1)} fusion(pred[256]{0:T(512)(128)(4,1)} %copy-done.10), kind=kLoop, calls=%fused_computation.42 | loop fusion | flops 196608 | bytes 65792 | tf_op jit(solution)/shard_map/and | solution.py:16
  56.1 1.8 %fusion.43 = f32[256,256]{1,0:T(8,128)} fusion(bf16[256,128]{1,0:T(8,128)(2,1)} %param.13, bf16[256,128]{1,0:T(8,128)(2,1)} %param.14), kind=kOutput, calls=%fused_computation.64 | convolution fusion | flops 16777216 | bytes 393216 | tf_op jit(solution)/shard_map/dot_general | solution.py:19
  57.9 1.0 broadcast_in_dim.97
  58.9 11.4 %while.17 = (s32[]{:T(128)}, f32[20,1024]{1,0:T(8,128)S(1)}, f32[8,20,1024]{2,1,0:T(8,128)}, f32[8,20,1024]{2,1,0:T(8,128)S(1)}, f32[8,20]{1,0:T(8,128)}, /*index=5*/s32[]{:T(128)}, s32[]{:T(128)}, s32[]{:T(128)}) while((s32[]{:T(128)}, f32[20,1024]{1,0:T(8,128)S(1)}, f32[8,20,1024]{2,1,0:T(8,128)}, f32[8,20,1024]{2,1,0:T(8,128)S(1)}, ...), condition=%wide.region_3.4_spmd.clone, body=%wide.region_2.3_spmd.clone.sunk | while | flops 81924 | bytes 426352 | solution.py:118
  60.3 0.7 fusion.55
  61.7 0.7 fusion.55
  63.1 0.7 fusion.55
  64.6 0.7 fusion.55
  66.0 0.7 fusion.55
  67.4 0.7 fusion.55
  68.9 0.7 fusion.55
  70.3 4.5 %all-to-all-start.1 = ((f32[20,8,1024]{2,0,1:T(8,128)}), f32[20,8,1024]{2,0,1:T(8,128)S(1)}, u32[]{:S(2)}, u32[]{:S(2)}) async-start(f32[20,8,1024]{2,0,1:T(8,128)} %bitcast.8), calls=%async_computation.1 | async-start | bytes 1572864 | tf_op jit(solution)/shard_map/all_to_all | solution.py:124
  74.8 2.8 %multiply_reduce_fusion.1 = f32[20,256]{1,0:T(8,128)} fusion(bf16[256,20,64]{0,2,1:T(8,128)(2,1)S(1)} %bitcast.81, f32[256,128]{0,1:T(8,128)} %copy-done.7, f32[1,20,64,128]{3,2,1,0:T(8,128)S(1)} %copy-done.2), kind=kOutput, calls=%fused_computation.17 | convolution fusion | flops 504622080 | bytes 1462272 | tf_op jit(solution)/shard_map/uhp,hpn->hun/dot_general | solution.py:35
  77.7 3.7 %fusion.21 = f32[256,20,64]{0,2,1:T(8,128)} fusion(bf16[256,20,64]{0,2,1:T(8,128)(2,1)S(1)} %bitcast.82, f32[256,256]{1,0:T(8,128)} %fusion.43, f32[20,256]{1,0:T(8,128)S(1)} %get-tuple-element.153, pred[256,256]{1,0:T(8,128)(4,1)} %fusion.37), kind=kOutput, calls=%fused_computation.29 | convolution fusion | flops 174325760 | bytes 2314240 | tf_op jit(solution)/shard_map/hsu,uhp->shp/dot_general | solution.py:24
  81.4 5.3 %multiply_reduce_fusion = (f32[20]{0:T(128)}, f32[20,256,256]{2,1,0:T(8,128)}) fusion(f32[20,256]{1,0:T(8,128)S(1)} %bitcast.86, f32[20,256]{1,0:T(8,128)S(1)} %copy-done.6, f32[256,256]{1,0:T(8,128)S(1)} %copy-done.5, f32[20,256]{1,0:T(8,128)S(1)} %get-tuple-element.153, pred[256,256]{1,0:T(8,128)(4,1)S(1)} %copy-done.8, ...), kind=kOutput, calls=%fused_computation.4 | convolution fusion | flops 179568624 | bytes 6942800 | tf_op jit(solution)/shard_map/shp,uhp->hsu/dot_general | solution.py:20
  86.8 5.5 %all-to-all-done.1 = f32[20,8,1024]{2,0,1:T(8,128)S(1)} async-done(((f32[20,8,1024]{2,0,1:T(8,128)}), f32[20,8,1024]{2,0,1:T(8,128)S(1)}, u32[]{:S(2)}, u32[]{:S(2)}) %all-to-all-start.1) | async-done | bytes 655392 | tf_op jit(solution)/shard_map/all_to_all | solution.py:124
  92.3 1.1 multiply_reduce_fusion.2
  93.4 2.8 %fusion.9 = (f32[20,256]{1,0:T(8,128)S(1)}, f32[20,128,256]{1,2,0:T(8,128)S(1)}) fusion(f32[256,128]{1,0:T(8,128)} %convert_element_type.21, f32[20,64,128]{2,1,0:T(8,128)S(1)} %reshape.294, bf16[256,20,64]{0,2,1:T(8,128)(2,1)S(1)} %bitcast.77), kind=kOutput, calls=%fused_computation.16 | convolution fusion | flops 504622080 | bytes 4083712 | tf_op jit(solution)/shard_map/shp,hpn->hsn/dot_general | solution.py:61
  96.5 5.2 %fusion.8 = f32[256,128]{1,0:T(8,128)} fusion(f32[20,128,256]{1,2,0:T(8,128)S(1)} %get-tuple-element.155, f32[20,256]{1,0:T(8,128)S(1)} %get-tuple-element.150, f32[20,256]{1,0:T(8,128)S(1)} %copy-done.6, f32[20,256,256]{2,1,0:T(8,128)} %get-tuple-element.157, f32[20,256]{1,0:T(8,128)S(1)} %get-tuple-element.153, pred[256,256]{1,0:T(8,128)(4,1)} %fusion.37, ...), kind=kOutput, calls=%fused_computation.15 | convolution fusion | flops 344686592 | bytes 8187904 | tf_op jit(solution)/shard_map/hsu,un->hsn/dot_general | solution.py:25
  101.8 0.7 fusion.25
  102.4 19.4 %psum.15 = f32[20]{0:T(128)S(1)} all-reduce(f32[20]{0:T(128)S(1)} %multiply_add_fusion), channel_id=1, replica_groups=mesh['seq'=8,'head'=4] {'seq'}, use_global_device_ids=true, to_apply=%region_12.13 | all-reduce | flops 20 | bytes 160 | tf_op jit(solution)/shard_map/psum | solution.py:143
  121.8 1.1 copy.44
  123.4 9.1 %all-reduce.3.cloned.1.call-done = f32[256,128]{1,0:T(8,128)} async-done(((f32[256,128]{1,0:T(8,128)}), f32[256,128]{1,0:T(8,128)}) %all-reduce.3.cloned.1.call-update) | async-done | bytes 131088 | tf_op jit(solution)/shard_map/psum | solution.py:142
  132.6 1.6 %copy.62 = f32[256,128]{1,0:T(8,128)} copy(f32[256,128]{1,0:T(8,128)} %all-reduce.3.cloned.1.call-done) | data formatting | bytes 262144
  (90 shorter events, 13.1 us)
Async XLA Ops:
  7.2 16.8 %copy-start.20 = (u32[32]{0:T(128)S(1)}, u32[32]{0:T(128)}, u32[]{:S(2)}) copy-start(u32[32]{0:T(128)} %constant.57) | copy-start | bytes 388
  7.2 45.2 %copy-start.3 = (bf16[256,128]{1,0:T(8,128)(2,1)S(1)}, bf16[256,128]{1,0:T(8,128)(2,1)}, u32[]{:S(2)}) copy-start(bf16[256,128]{1,0:T(8,128)(2,1)} %param.13) | copy-start | bytes 196612
  7.2 45.8 %copy-start.1 = (bf16[256,1280]{1,0:T(8,128)(2,1)S(1)}, bf16[256,1280]{1,0:T(8,128)(2,1)}, u32[]{:S(2)}) copy-start(bf16[256,1280]{1,0:T(8,128)(2,1)} %param.10) | copy-start | bytes 1966084
  7.2 46.0 %copy-start.2 = (f32[1,20,64,128]{3,2,1,0:T(8,128)S(1)}, f32[1,20,64,128]{3,2,1,0:T(8,128)}, u32[]{:S(2)}) copy-start(f32[1,20,64,128]{3,2,1,0:T(8,128)} %param.16) | copy-start | bytes 1966084
  8.6 43.7 %copy-start.14 = (f32[20]{0:T(128)}, f32[20]{0:T(128)S(1)}, u32[]{:S(2)}) copy-start(f32[20]{0:T(128)S(1)} %neg.7) | copy-start | bytes 244
  10.9 41.4 %copy-start.10 = (pred[256]{0:T(512)(128)(4,1)}, pred[256]{0:T(512)(128)(4,1)S(1)}, u32[]{:S(2)}) copy-start(pred[256]{0:T(512)(128)(4,1)S(1)} %get-tuple-element.158) | copy-start | bytes 772
  11.2 41.1 %copy-start.11 = (f32[20]{0:T(128)}, f32[20]{0:T(128)S(1)}, u32[]{:S(2)}) copy-start(f32[20]{0:T(128)S(1)} %get-tuple-element.137) | copy-start | bytes 244
  12.2 1.4 copy-start.7
  16.7 41.2 %all-to-all-start = ((f32[20,8,1024]{2,0,1:T(8,128)}), f32[20,8,1024]{2,0,1:T(8,128)S(1)}, u32[]{:S(2)}, u32[]{:S(2)}) async-start(f32[20,8,1024]{2,0,1:T(8,128)} %copy.39), calls=%async_computation | async-start | bytes 1572864 | tf_op jit(solution)/shard_map/all_to_all | solution.py:116
  70.3 22.0 %all-to-all-start.1 = ((f32[20,8,1024]{2,0,1:T(8,128)}), f32[20,8,1024]{2,0,1:T(8,128)S(1)}, u32[]{:S(2)}, u32[]{:S(2)}) async-start(f32[20,8,1024]{2,0,1:T(8,128)} %bitcast.8), calls=%async_computation.1 | async-start | bytes 1572864 | tf_op jit(solution)/shard_map/all_to_all | solution.py:124
  74.8 57.8 %all-reduce.3.cloned.1.call-start = ((), (), s32[]{:S(2)}) async-start(), calls=%async_computation.2 | async-start | bytes 262144 | tf_op jit(solution)/shard_map/psum | solution.py:142
  77.7 3.7 %copy-start.5 = (f32[256,256]{1,0:T(8,128)S(1)}, f32[256,256]{1,0:T(8,128)}, u32[]{:S(2)}) copy-start(f32[256,256]{1,0:T(8,128)} %fusion.43) | copy-start | bytes 786436
  77.7 3.7 %copy-start.6 = (f32[20,256]{1,0:T(8,128)S(1)}, f32[20,256]{1,0:T(8,128)}, u32[]{:S(2)}) copy-start(f32[20,256]{1,0:T(8,128)} %param.11) | copy-start | bytes 61444
  77.7 3.7 %copy-start.8 = (pred[256,256]{1,0:T(8,128)(4,1)S(1)}, pred[256,256]{1,0:T(8,128)(4,1)}, u32[]{:S(2)}) copy-start(pred[256,256]{1,0:T(8,128)(4,1)} %fusion.37) | copy-start | bytes 196612
  86.8 9.4 %copy-start.9 = (f32[20,256]{1,0:T(8,128)S(1)}, f32[20,256]{1,0:T(8,128)}, u32[]{:S(2)}) copy-start(f32[20,256]{1,0:T(8,128)} %multiply_reduce_fusion.1) | copy-start | bytes 61444
  86.8 9.4 %copy-start.12 = (f32[20]{0:T(128)S(1)}, f32[20]{0:T(128)}, u32[]{:S(2)}) copy-start(f32[20]{0:T(128)} %copy-done.11) | copy-start | bytes 244
  86.8 9.5 %copy-start.13 = (f32[20]{0:T(128)S(1)}, f32[20]{0:T(128)}, u32[]{:S(2)}) copy-start(f32[20]{0:T(128)} %slice_reduce_fusion.1) | copy-start | bytes 244
  86.8 9.5 %copy-start.15 = (f32[20]{0:T(128)S(1)}, f32[20]{0:T(128)}, u32[]{:S(2)}) copy-start(f32[20]{0:T(128)} %copy-done.14) | copy-start | bytes 244
  86.8 9.5 %copy-start.16 = (pred[256]{0:T(512)(128)(4,1)S(1)}, pred[256]{0:T(512)(128)(4,1)}, u32[]{:S(2)}) copy-start(pred[256]{0:T(512)(128)(4,1)} %get-tuple-element.159) | copy-start | bytes 772
  86.8 9.5 %copy-start.18 = (pred[256]{0:T(512)(128)(4,1)S(1)}, pred[256]{0:T(512)(128)(4,1)}, u32[]{:S(2)}) copy-start(pred[256]{0:T(512)(128)(4,1)} %compare_bitcast_fusion) | copy-start | bytes 772
  96.5 5.2 %copy-start.17 = (f32[20]{0:T(128)S(1)}, f32[20]{0:T(128)}, u32[]{:S(2)}) copy-start(f32[20]{0:T(128)} %get-tuple-element.148) | copy-start | bytes 244
  96.5 5.2 %copy-start.19 = (f32[20]{0:T(128)S(1)}, f32[20]{0:T(128)}, u32[]{:S(2)}) copy-start(f32[20]{0:T(128)} %get-tuple-element.156) | copy-start | bytes 244
  96.5 5.2 %copy-start = (f32[256,20,64]{0,2,1:T(8,128)S(1)}, f32[256,20,64]{0,2,1:T(8,128)}, u32[]{:S(2)}) copy-start(f32[256,20,64]{0,2,1:T(8,128)} %fusion.21) | copy-start | bytes 3932164
  96.5 5.2 %copy-start.4 = (bf16[256,128]{1,0:T(8,128)(2,1)S(1)}, bf16[256,128]{1,0:T(8,128)(2,1)}, u32[]{:S(2)}) copy-start(bf16[256,128]{1,0:T(8,128)(2,1)} %param.13) | copy-start | bytes 196612
Sparse Core Ops, SparseCore 0:
  101.8 30.7 all-reduce.2
where the time goes:
time: 142 us; the launch traced here: 141 us
  blocking collectives  45.5 us (32%)
  matrix products  24 us (17%)
  local copies, waits for them, and re-layouts  16.6 us (12%)
  between operations  15.8 us (11%)
  waiting for transfers between devices  14.6 us (10%)
  other arithmetic  12.4 us (9%)
  starting transfers between devices  11.9 us (8%)
    unnamed x1, blocking collectives  26.1 us
    psum x1, blocking collectives, body(): grad_rate = -lax.psum(rate_total, 'seq')  19.4 us
    psum x1, waiting for transfers between devices, body(): grad_input_map = lax.psum(grad_b_list[0], 'head')  9.15 us
    all_to_all x1, starting transfers between devices, body(): lax.all_to_all(sliced, 'seq', split_axis=1, concat_axis=1, tiled=True)  7.31 us
    mul x8, local copies, waits for them, and re-layouts, backward_step(): return (grad_piece + gain_piece[:, None] * running, running)  5.48 us
    all_to_all x1, waiting for transfers between devices, body(): lax.all_to_all(jnp.transpose(exclusive, (1, 0, 2)), 'seq', split_axis=1,...  5.48 us
    dot_general x1, matrix products, prepare(): jnp.einsum('shp,uhp->hsu', x_block, grad_block, preferred_element_type=jn...  5.34 us
    unnamed x51, local copies, waits for them, and re-layouts  5.26 us
  transfers between devices with their start and end apart: 3, of which 2 were waited for; matrix products, arithmetic and copies ran while one was open for 15% of the time, Pallas kernels for 0%

commit v1 on v0

--- a/solution.py
+++ b/solution.py
@@ -2,6 +2,7 @@
 import jax.numpy as jnp
 from jax import lax
 from jax.sharding import PartitionSpec as P
+from jax.lax import all_to_all, axis_size
 
 highest = lax.Precision.HIGHEST
 
@@ -113,7 +114,9 @@
     seq_count = lax.axis_size("seq")
     entries = grad_total.shape[1] * grad_total.shape[2]
     sliced = grad_total.reshape(head_count, seq_count, entries // seq_count)
-    received = lax.all_to_all(sliced, "seq", split_axis=1, concat_axis=1, tiled=True)
+    received = jnp.concatenate(
+        all_to_all(jnp.stack(jnp.split(sliced, axis_size("seq"), axis=1), 0), "seq", 0, 0), 1
+    )
     gains = lax.all_gather(gain_total[None], "seq", axis=0, tiled=True)
     ending, exclusive = lax.scan(
         backward_step,

time: 142 us -> 135 us (0.951)
  blocking collectives: 45.5 us -> 43.5 us
    unnamed x51 -> x56, local copies, waits for them, and re-layouts: 5.26 us -> 10.9 us
    mul x8, local copies, waits for them, and re-layouts: 5.48 us -> 0.06 us  [backward_step(): return (grad_piece + gain_piece[:, None] * running, running)]
    unnamed x1, blocking collectives: 26.1 us -> 24.1 us
where the time goes in v1:
time: 135 us
  blocking collectives  43.5 us (32%)
  matrix products  23.4 us (17%)
  between operations  15.8 us (12%)
  local copies, waits for them, and re-layouts  15.2 us (11%)
  waiting for transfers between devices  13.5 us (10%)
  other arithmetic  11.9 us (9%)
  starting transfers between devices  11.1 us (8%)
    unnamed x1, blocking collectives  24.1 us
    psum x1, blocking collectives, body(): grad_rate = -lax.psum(rate_total, 'seq')  19.4 us
    unnamed x56, local copies, waits for them, and re-layouts  10.9 us
    psum x1, waiting for transfers between devices, body(): grad_input_map = lax.psum(grad_b_list[0], 'head')  9.15 us
    all_to_all x1, starting transfers between devices, body(): all_to_all(jnp.stack(jnp.split(sliced, axis_size('seq'), axis=1), 0), 'se...  7.31 us
    dot_general x1, matrix products, prepare(): jnp.einsum('shp,uhp->hsu', x_block, grad_block, preferred_element_type=jn...  6.15 us
    dynamic_update_slice x8, other arithmetic, body(): lax.scan(backward_step, jnp.zeros_like(received[:, 0]), (jnp.transpose(re...  5.16 us
    dot_general x1, matrix products, prepare(): jnp.einsum('hsu,un->hsn', paired, c_block, preferred_element_type=jnp.flo...  5.16 us
  transfers between devices with their start and end apart: 3, of which 2 were waited for; matrix products, arithmetic and copies ran while one was open for 15% of the time, Pallas kernels for 0%

profile of v1, /device:TPU:0, one launch (start us, length us, event | category | flops | bytes accessed | tf_op | source)
XLA Modules:
  0.0 134.6 jit_solution(3752591402788101955)
XLA Ops:
  8.6 0.8 reshape.296
  10.6 0.9 copy.61
  11.6 1.4 %copy.60 = bf16[256,1280]{0,1:T(8,128)(2,1)S(1)} copy(bf16[256,1280]{1,0:T(8,128)(2,1)} %param.15) | data formatting | bytes 1310720 | tf_op args[5]
  13.0 0.8 copy-done.3
  13.8 1.7 %fusion.31 = f32[20,64,128]{2,1,0:T(8,128)S(1)} fusion(bf16[256,20,64]{0,2,1:T(8,128)(2,1)S(1)} %bitcast.117, f32[256,128]{0,1:T(8,128)S(1)} %copy.61, f32[20,256]{1,0:T(8,128)S(1)} %get-tuple-element.160, f32[20]{0:T(128)S(1)} %broadcast_multiply_fusion.1), kind=kOutput, calls=%fused_computation.38 | convolution fusion | flops 504135680 | bytes 1462352 | tf_op jit(solution)/shard_map/hun,uhp->hpn/dot_general | solution.py:35
  16.3 0.7 fusion.44
  17.0 0.7 fusion.43
  17.7 0.7 fusion.42
  18.4 0.7 fusion.41
  19.1 0.7 fusion.40
  19.8 0.7 fusion.39
  20.5 0.7 fusion.38
  21.2 7.3 %all-to-all-start = ((f32[8,20,1,1024]{3,2,1,0:T(1,128)}), f32[8,20,1,1024]{3,2,1,0:T(1,128)S(1)}, u32[]{:S(2)}, u32[]{:S(2)}) async-start(f32[8,20,1,1024]{3,2,1,0:T(1,128)} %fusion.38), calls=%async_computation | async-start | bytes 1310720 | tf_op jit(solution)/shard_map/all_to_all | solution.py:118
  30.0 24.1 %all-reduce = f32[160]{0:T(256)S(1)} all-reduce(f32[160]{0:T(256)S(1)} %dynamic-update-slice), channel_id=2, replica_groups=mesh['seq'=8,'head'=4] {'seq'}, use_global_device_ids=true, to_apply=%add | all-reduce | flops 160 | bytes 1280
  55.9 0.7 fusion.37
  56.7 0.9 fusion.51
  57.7 1.0 broadcast_in_dim.97
  58.7 6.1 %while.17 = (s32[]{:T(128)}, f32[20,1024]{1,0:T(8,128)S(1)}, f32[8,20,1024]{2,1,0:T(8,128)}, f32[8,20,1024]{2,1,0:T(8,128)S(1)}, f32[8,20]{1,0:T(8,128)S(1)}, /*index=5*/s32[]{:T(128)}, s32[]{:T(128)}, s32[]{:T(128)}) while((s32[]{:T(128)}, f32[20,1024]{1,0:T(8,128)S(1)}, f32[8,20,1024]{2,1,0:T(8,128)}, ...), condition=%wide.region_3.4_spmd.clone, body=%wide.region_2.3_spmd.clone.sunk | while | flops 81924 | bytes 426352 | solution.py:121
  64.8 3.7 %all-to-all-start.1 = ((f32[20,8,1024]{2,0,1:T(8,128)}), f32[20,8,1024]{2,0,1:T(8,128)S(1)}, u32[]{:S(2)}, u32[]{:S(2)}) async-start(f32[20,8,1024]{2,0,1:T(8,128)} %bitcast.19), calls=%async_computation.1 | async-start | bytes 1572864 | tf_op jit(solution)/shard_map/all_to_all | solution.py:127
  68.6 3.0 %multiply_reduce_fusion.1 = f32[20,256]{1,0:T(8,128)} fusion(bf16[256,20,64]{0,2,1:T(8,128)(2,1)} %bitcast.118, f32[256,128]{0,1:T(8,128)} %copy-done.14, f32[1,20,64,128]{3,2,1,0:T(8,128)S(1)} %copy-done.2), kind=kOutput, calls=%fused_computation.17 | convolution fusion | flops 504622080 | bytes 1462272 | tf_op jit(solution)/shard_map/uhp,hpn->hun/dot_general | solution.py:36
  71.6 3.9 %fusion.21 = f32[256,20,64]{0,2,1:T(8,128)} fusion(bf16[256,20,64]{0,2,1:T(8,128)(2,1)} %bitcast.119, f32[256,256]{1,0:T(8,128)S(1)} %copy-done.10, f32[20,256]{1,0:T(8,128)S(1)} %get-tuple-element.161, pred[256,256]{1,0:T(8,128)(4,1)S(1)} %copy-done.15), kind=kOutput, calls=%fused_computation.29 | convolution fusion | flops 174325760 | bytes 2314240 | tf_op jit(solution)/shard_map/hsu,uhp->shp/dot_general | solution.py:25
  75.6 6.2 %multiply_reduce_fusion = (f32[20]{0:T(128)}, f32[20,256,256]{2,1,0:T(8,128)}) fusion(f32[20,256]{1,0:T(8,128)S(1)} %bitcast.124, f32[20,256]{1,0:T(8,128)S(1)} %copy-done.12, f32[256,256]{1,0:T(8,128)S(1)} %copy-done.10, f32[20,256]{1,0:T(8,128)} %copy-done.16, pred[256,256]{1,0:T(8,128)(4,1)S(1)} %copy-done.15, bf16[256,20,64]{0,2,1:T(8,128)(2,1)S(1)} %bitcast.113, ...), kind=kOutput, calls=%fused_computation.4 | convolution fusion | flops 179568624 | bytes 6942800 | tf_op jit(solution)/shard_map/shp,uhp->hsu/dot_general | solution.py:21
  81.7 4.3 %all-to-all-done.1 = f32[20,8,1024]{2,0,1:T(8,128)S(1)} async-done(((f32[20,8,1024]{2,0,1:T(8,128)}), f32[20,8,1024]{2,0,1:T(8,128)S(1)}, u32[]{:S(2)}, u32[]{:S(2)}) %all-to-all-start.1) | async-done | bytes 655392 | tf_op jit(solution)/shard_map/all_to_all | solution.py:127
  86.0 1.1 multiply_reduce_fusion.2
  87.2 1.9 %fusion.9 = (f32[20,256]{1,0:T(8,128)S(1)}, f32[20,128,256]{1,2,0:T(8,128)S(1)}) fusion(f32[256,128]{1,0:T(8,128)S(1)} %copy-done.7, f32[20,64,128]{2,1,0:T(8,128)S(1)} %reshape.302, bf16[256,20,64]{0,2,1:T(8,128)(2,1)S(1)} %bitcast.114), kind=kOutput, calls=%fused_computation.16 | convolution fusion | flops 504622080 | bytes 4083712 | tf_op jit(solution)/shard_map/shp,hpn->hsn/dot_general | solution.py:62
  89.1 1.0 multiply_reduce_fusion.4
  90.1 5.2 %fusion.8 = f32[256,128]{1,0:T(8,128)} fusion(f32[20,128,256]{1,2,0:T(8,128)S(1)} %get-tuple-element.163, f32[20,256]{1,0:T(8,128)S(1)} %get-tuple-element.158, f32[20,256]{1,0:T(8,128)} %param.11, f32[20,256,256]{2,1,0:T(8,128)} %get-tuple-element.165, f32[20,256]{1,0:T(8,128)} %copy-done.16, pred[256,256]{1,0:T(8,128)(4,1)} %fusion.37, ...), kind=kOutput, calls=%fused_computation.15 | convolution fusion | flops 344686592 | bytes 8187904 | tf_op jit(solution)/shard_map/hsu,un->hsn/dot_general | solution.py:26
  95.4 0.7 fusion.25
  96.1 19.4 %psum.15 = f32[20]{0:T(128)S(1)} all-reduce(f32[20]{0:T(128)S(1)} %multiply_add_fusion), channel_id=1, replica_groups=mesh['seq'=8,'head'=4] {'seq'}, use_global_device_ids=true, to_apply=%region_12.13 | all-reduce | flops 20 | bytes 160 | tf_op jit(solution)/shard_map/psum | solution.py:146
  115.5 1.1 copy.69
  117.0 9.1 %all-reduce.3.cloned.1.call-done = f32[256,128]{1,0:T(8,128)} async-done(((f32[256,128]{1,0:T(8,128)}), f32[256,128]{1,0:T(8,128)}) %all-reduce.3.cloned.1.call-update) | async-done | bytes 131088 | tf_op jit(solution)/shard_map/psum | solution.py:145
  126.2 1.6 %copy.97 = f32[256,128]{1,0:T(8,128)} copy(f32[256,128]{1,0:T(8,128)} %all-reduce.3.cloned.1.call-done) | data formatting | bytes 262144
  (96 shorter events, 12.0 us)
Async XLA Ops:
  7.2 21.4 %copy-start.19 = (u32[32]{0:T(128)S(1)}, u32[32]{0:T(128)}, u32[]{:S(2)}) copy-start(u32[32]{0:T(128)} %constant.57) | copy-start | bytes 388
  7.2 47.0 %copy-start.5 = (bf16[256,128]{1,0:T(8,128)(2,1)S(1)}, bf16[256,128]{1,0:T(8,128)(2,1)}, u32[]{:S(2)}) copy-start(bf16[256,128]{1,0:T(8,128)(2,1)} %param.13) | copy-start | bytes 196612
  7.2 47.7 %copy-start.1 = (bf16[256,1280]{1,0:T(8,128)(2,1)S(1)}, bf16[256,1280]{1,0:T(8,128)(2,1)}, u32[]{:S(2)}) copy-start(bf16[256,1280]{1,0:T(8,128)(2,1)} %param.10) | copy-start | bytes 1966084
  7.2 47.9 %copy-start.2 = (f32[1,20,64,128]{3,2,1,0:T(8,128)S(1)}, f32[1,20,64,128]{3,2,1,0:T(8,128)}, u32[]{:S(2)}) copy-start(f32[1,20,64,128]{3,2,1,0:T(8,128)} %param.16) | copy-start | bytes 1966084
  10.3 47.2 %copy-start.8 = (f32[3,8,2,128]{3,1,2,0:T(8,128)}, f32[3,8,2,128]{3,1,2,0:T(8,128)S(1)}, u32[]{:S(2)}) copy-start(f32[3,8,2,128]{3,1,2,0:T(8,128)S(1)} %copy.73) | copy-start | bytes 73732
  10.3 46.3 %copy-start.11 = (bf16[256,128]{1,0:T(8,128)(2,1)S(1)}, bf16[256,128]{1,0:T(8,128)(2,1)}, u32[]{:S(2)}) copy-start(bf16[256,128]{1,0:T(8,128)(2,1)} %param.14) | copy-start | bytes 196612
  10.4 61.2 %copy-start.16 = (f32[20,256]{1,0:T(8,128)}, f32[20,256]{1,0:T(8,128)S(1)}, u32[]{:S(2)}) copy-start(f32[20,256]{1,0:T(8,128)S(1)} %get-tuple-element.161) | copy-start | bytes 61444
  11.6 9.6 %copy-start.14 = (f32[256,128]{0,1:T(8,128)}, f32[256,128]{0,1:T(8,128)S(1)}, u32[]{:S(2)}) copy-start(f32[256,128]{0,1:T(8,128)S(1)} %copy.61) | copy-start | bytes 393220
  13.0 0.8 copy-start.3
  21.2 36.3 %all-to-all-start = ((f32[8,20,1,1024]{3,2,1,0:T(1,128)}), f32[8,20,1,1024]{3,2,1,0:T(1,128)S(1)}, u32[]{:S(2)}, u32[]{:S(2)}) async-start(f32[8,20,1,1024]{3,2,1,0:T(1,128)} %fusion.38), calls=%async_computation | async-start | bytes 1310720 | tf_op jit(solution)/shard_map/all_to_all | solution.py:118
  57.7 13.9 %copy-start.10 = (f32[256,256]{1,0:T(8,128)S(1)}, f32[256,256]{1,0:T(8,128)}, u32[]{:S(2)}) copy-start(f32[256,256]{1,0:T(8,128)} %fusion.51) | copy-start | bytes 786436
  57.7 13.9 %copy-start.15 = (pred[256,256]{1,0:T(8,128)(4,1)S(1)}, pred[256,256]{1,0:T(8,128)(4,1)}, u32[]{:S(2)}) copy-start(pred[256,256]{1,0:T(8,128)(4,1)} %fusion.37) | copy-start | bytes 196612
  64.8 21.3 %all-to-all-start.1 = ((f32[20,8,1024]{2,0,1:T(8,128)}), f32[20,8,1024]{2,0,1:T(8,128)S(1)}, u32[]{:S(2)}, u32[]{:S(2)}) async-start(f32[20,8,1024]{2,0,1:T(8,128)} %bitcast.19), calls=%async_computation.1 | async-start | bytes 1572864 | tf_op jit(solution)/shard_map/all_to_all | solution.py:127
  68.5 57.7 %all-reduce.3.cloned.1.call-start = ((), (), s32[]{:S(2)}) async-start(), calls=%async_computation.2 | async-start | bytes 262144 | tf_op jit(solution)/shard_map/psum | solution.py:145
  71.6 3.9 %copy-start.4 = (bf16[256,1280]{0,1:T(8,128)(2,1)S(1)}, bf16[256,1280]{0,1:T(8,128)(2,1)}, u32[]{:S(2)}) copy-start(bf16[256,1280]{0,1:T(8,128)(2,1)} %copy-done.3) | copy-start | bytes 1966084
  71.6 3.9 %copy-start.9 = (f32[3,8,2,128]{3,1,2,0:T(8,128)S(1)}, f32[3,8,2,128]{3,1,2,0:T(8,128)}, u32[]{:S(2)}) copy-start(f32[3,8,2,128]{3,1,2,0:T(8,128)} %copy-done.8) | copy-start | bytes 73732
  71.6 3.9 %copy-start.12 = (f32[20,256]{1,0:T(8,128)S(1)}, f32[20,256]{1,0:T(8,128)}, u32[]{:S(2)}) copy-start(f32[20,256]{1,0:T(8,128)} %param.11) | copy-start | bytes 61444
  75.5 11.6 %copy-start.7 = (f32[256,128]{1,0:T(8,128)S(1)}, f32[256,128]{1,0:T(8,128)}, u32[]{:S(2)}) copy-start(f32[256,128]{1,0:T(8,128)} %convert_element_type.21) | copy-start | bytes 393220
  90.1 5.2 %copy-start.17 = (f32[20]{0:T(128)S(1)}, f32[20]{0:T(128)}, u32[]{:S(2)}) copy-start(f32[20]{0:T(128)} %get-tuple-element.156) | copy-start | bytes 244
  90.1 5.2 %copy-start.18 = (f32[20]{0:T(128)S(1)}, f32[20]{0:T(128)}, u32[]{:S(2)}) copy-start(f32[20]{0:T(128)} %get-tuple-element.164) | copy-start | bytes 244
  90.1 5.3 %copy-start = (f32[256,20,64]{0,2,1:T(8,128)S(1)}, f32[256,20,64]{0,2,1:T(8,128)}, u32[]{:S(2)}) copy-start(f32[256,20,64]{0,2,1:T(8,128)} %fusion.21) | copy-start | bytes 3932164
  90.1 5.3 %copy-start.6 = (bf16[256,128]{1,0:T(8,128)(2,1)S(1)}, bf16[256,128]{1,0:T(8,128)(2,1)}, u32[]{:S(2)}) copy-start(bf16[256,128]{1,0:T(8,128)(2,1)} %param.13) | copy-start | bytes 196612
  90.1 5.3 %copy-start.13 = (f32[20,256]{1,0:T(8,128)S(1)}, f32[20,256]{1,0:T(8,128)}, u32[]{:S(2)}) copy-start(f32[20,256]{1,0:T(8,128)} %param.11) | copy-start | bytes 61444
Sparse Core Ops, SparseCore 0:
  95.4 30.7 all-reduce.2
